TPU v7x, 32 devices: a whole 2x2x4 slice. The times are simulated.
32 devices in a mesh: dp: 8 (over y, x, core), mp: 4 (over z).
Axes of the slice: x: 2, y: 2, z: 4, core: 2. Of those that a mesh axis runs over, the one named last changes fastest.
Arguments:
- states: bfloat16 [128, 80, 768], P('dp'), may hold values from -6 to 6
- hist_len: int32 [128], P('dp'), may hold values from 1 to 20
- norm_gain: float32 [768], replicated, may hold values from 0.5 to 1.5
- qkv_weight: bfloat16 [768, 3, 12, 64], P(None, None, 'mp'), may hold values from -1 to 1
- output_weight: bfloat16 [12, 64, 768], P('mp'), may hold values from -0.21875 to 0.21875
- cotangent: bfloat16 [128, 80, 768], P('dp'), may hold values from -6 to 6
Outputs:
- attended: bfloat16 [128, 80, 768], P('dp')
- grad_states: bfloat16 [128, 80, 768], P('dp')
- grad_qkv: float32 [768, 3, 12, 64], P('dp', None, 'mp')
- output_weight_gradient: float32 [12, 64, 768], P('mp', None, 'dp')
- grad_gain: float32 [768], P('dp')
All inputs are finite; a program needn't handle non-finite values.
Results may differ from a plain program's by a relative error of at most 0.012.
Values may be sent and summed in bfloat16 or wider, within the bound.
A program may use at most 128 MiB of HBM per device.

v0:
```python
import jax
import jax.numpy as jnp
from jax import lax
from jax.sharding import PartitionSpec as P

LEVELS = 4


def body(states, hist_len, norm_gain, qkv_weight, output_weight, cotangent):
    wide_states = states.astype(jnp.float32)
    inv_rms = lax.rsqrt(jnp.mean(wide_states * wide_states, axis=-1, keepdims=True) + 1e-06)
    unit = wide_states * inv_rms
    normed = (unit * norm_gain).astype(jnp.bfloat16)
    proj = jnp.einsum(
        "bsd,dchk->bschk", normed, qkv_weight, preferred_element_type=jnp.float32
    ).astype(jnp.bfloat16)
    queries = proj[:, :, 0]
    key_rows = proj[:, :, 1]
    value_rows = proj[:, :, 2]
    positions = jnp.arange(states.shape[1], dtype=jnp.int32)
    keep_mask = positions[None, :] < LEVELS * hist_len[:, None]
    scores = jnp.einsum("bqhk,bphk->bhqp", queries, key_rows, preferred_element_type=jnp.float32)
    masked = jnp.where(keep_mask[:, None, None, :], scores, -1e30)
    row_top = jnp.max(masked, axis=-1, keepdims=True)
    exp_scores = jnp.exp(masked - row_top)
    attn_prob = exp_scores / jnp.sum(exp_scores, axis=-1, keepdims=True)
    prob_bf = attn_prob.astype(jnp.bfloat16)
    attended_context = jnp.einsum(
        "bhqp,bphk->bqhk", prob_bf, value_rows, preferred_element_type=jnp.float32
    ).astype(jnp.bfloat16)
    partial_mix = jnp.einsum(
        "zagm,gms->zas", attended_context, output_weight, preferred_element_type=jnp.float32
    )
    mixed_total_sum = lax.psum(partial_mix.astype(jnp.bfloat16), "mp").astype(jnp.float32)
    attended = (wide_states + mixed_total_sum).astype(jnp.bfloat16)
    masked_cotangent = jnp.where(keep_mask[:, :, None], cotangent, jnp.zeros_like(cotangent))
    local_output = jnp.einsum(
        "wmep,wmx->epx", attended_context, masked_cotangent, preferred_element_type=jnp.float32
    )
    context_gradient = jnp.einsum(
        "uxy,wgy->uxwg", masked_cotangent, output_weight, preferred_element_type=jnp.float32
    ).astype(jnp.bfloat16)
    grad_prob = jnp.einsum(
        "bqhk,bphk->bhqp", context_gradient, value_rows, preferred_element_type=jnp.float32
    )
    row_delta = jnp.sum(attn_prob * grad_prob, axis=-1, keepdims=True)
    grad_score = (attn_prob * (grad_prob - row_delta)).astype(jnp.bfloat16)
    grad_query = jnp.einsum(
        "bhqp,bphk->bqhk", grad_score, key_rows, preferred_element_type=jnp.float32
    )
    grad_key = jnp.einsum(
        "bhqp,bqhk->bphk", grad_score, queries, preferred_element_type=jnp.float32
    )
    grad_value = jnp.einsum(
        "bhqp,bqhk->bphk", prob_bf, context_gradient, preferred_element_type=jnp.float32
    )
    grad_proj = jnp.stack([grad_query, grad_key, grad_value], axis=2).astype(jnp.bfloat16)
    local_qkv = jnp.einsum("bsd,bschk->dchk", normed, grad_proj, preferred_element_type=jnp.float32)
    partial_normed = jnp.einsum(
        "bschk,dchk->bsd", grad_proj, qkv_weight, preferred_element_type=jnp.float32
    )
    wide_cot = masked_cotangent.astype(jnp.float32)
    grad_normed = lax.psum(partial_normed, "mp")
    local_gain = jnp.sum(grad_normed * unit, axis=(0, 1))
    unit_grad = grad_normed * norm_gain
    row_corr = jnp.mean(unit_grad * unit, axis=-1, keepdims=True)
    grad_states = (wide_cot + inv_rms * (unit_grad - unit * row_corr)).astype(jnp.bfloat16)
    grad_qkv, output_weight_gradient, grad_gain = (
        lax.psum_scatter(local_qkv, "dp", scatter_dimension=0, tiled=True),
        lax.psum_scatter(local_output, "dp", scatter_dimension=2, tiled=True),
        lax.psum_scatter(local_gain, "dp", scatter_dimension=0, tiled=True),
    )
    return (attended, grad_states, grad_qkv, output_weight_gradient, grad_gain)


def solution(mesh):
    placed = (
        P("dp", None, None),
        P("dp"),
        P(),
        P(None, None, "mp", None),
        P("mp", None, None),
        P("dp", None, None),
    )
    return jax.shard_map(
        body,
        mesh=mesh,
        in_specs=placed,
        out_specs=(
            P("dp", None, None),
            P("dp", None, None),
            P("dp", None, "mp", None),
            P("mp", None, "dp"),
            P("dp"),
        ),
        check_vma=False,
    )
```

profile of v0, /device:TPU:0, one launch (start us, length us, event | category | flops | bytes accessed | tf_op | source)
XLA Modules:
  0.0 289.7 jit_solution(6222700549356190898)
XLA Ops:
  8.0 0.0 copy-start
  8.0 0.0 copy-start.1
  8.0 0.0 reduce-scatter.9.cloned.1.call-start
  8.1 0.8 broadcast_multiply_fusion.1
  8.9 0.1 iota_compare_fusion
  9.0 2.0 fusion.12
  11.0 3.4 %convolution_convert_fusion = bf16[16,80,3,3,64]{1,4,3,2,0:T(8,128)(2,1)} fusion(bf16[16,80,768]{2,1,0:T(8,128)(2,1)S(1)} %copy-done.1, f32[768]{0:T(1024)S(1)} %copy-done.9, f32[16,80]{1,0:T(8,128)S(1)} %add_rsqrt_fusion, bf16[768,3,3,64]{0,3,2,1:T(8,128)(2,1)S(1)} %copy-done), kind=kOutput, calls=%fused_computation.20 | convolution fusion | flops 1137131520 | bytes 4333568 | tf_op jit(solution)/shard_map/bsd,dchk->bschk/dot_general | solution.py:14
  14.5 3.6 %fusion.51 = (f32[16,3,80]{2,1,0:T(4,128)S(1)}, f32[16,3,80,80]{2,3,1,0:T(8,128)}) fusion(pred[16,80]{1,0:T(8,128)(4,1)S(1)} %iota_compare_fusion, bf16[16,80,3,3,64]{1,4,3,2,0:T(8,128)(2,1)} %convolution_convert_fusion), kind=kOutput, calls=%fused_computation.69 | convolution fusion | flops 40243280 | bytes 2818304 | tf_op jit(solution)/shard_map/sub | solution.py:25
  18.1 2.3 fusion.27
  20.4 0.0 copy-start.5
  20.4 0.9 copy-done.5
  21.4 0.9 fusion.31
  22.3 1.5 copy.40
  23.8 2.7 reshape.73
  26.5 0.0 reduce-scatter.9.cloned.1.call-update
  26.5 0.0 reduce-scatter.7.cloned.1.call-start
  26.6 0.0 copy-done.8
  26.6 0.0 copy-start.3
  26.6 2.6 fusion.24
  29.2 0.6 fusion.30
  29.9 1.0 copy-done.4
  30.9 0.6 multiply_reduce_fusion
  31.5 0.5 multiply_convert_fusion
  32.0 0.4 fusion.28
  32.4 0.6 fusion.29
  33.0 0.0 copy-done.11
  33.0 3.0 %fusion.14 = f32[768,3,3,64,1]{0,3,2,4,1:T(8,128)} fusion(bf16[16,80,768]{2,1,0:T(8,128)(2,1)S(1)} %copy-done.1, f32[768]{0:T(1024)S(1)} %copy-done.9, f32[16,80]{1,0:T(8,128)S(1)} %add_rsqrt_fusion, bf16[16,80,1,3,64]{1,4,3,0,2:T(8,128)(2,1)S(1)} %fusion.30, bf16[16,80,1,3,64]{1,4,3,0,2:T(8,128)(2,1)S(1)} %fusion.29, ...), kind=kOutput, calls=%fused_computation.21 | convolution fusion | flops 1140817920 | bytes 5218304 | tf_op jit(solution)/shard_map/bsd,bschk->dchk/dot_general | solution.py:58
  36.0 2.8 copy.42
  38.8 0.0 reduce-scatter.7.cloned.1.call-update
  38.9 0.0 all-reduce.6.cloned.1.call-start
  38.9 5.4 %convolution_bitcast_fusion = f32[16,80,768]{2,1,0:T(8,128)} fusion(bf16[16,80,1,3,64]{1,4,3,0,2:T(8,128)(2,1)} %copy-done.11, bf16[16,80,1,3,64]{1,4,3,0,2:T(8,128)(2,1)} %copy-done.7, bf16[16,80,1,3,64]{1,4,3,0,2:T(8,128)(2,1)} %copy-done.6, bf16[768,3,3,64]{0,3,2,1:T(8,128)(2,1)S(1)} %copy-done), kind=kOutput, calls=%fused_computation.19 | convolution fusion | flops 1133936640 | bytes 6291456 | tf_op jit(solution)/shard_map/bschk,dchk->bsd/dot_general | solution.py:59
  44.3 0.0 all-reduce.6.cloned.1.call-update
  44.3 0.0 copy-start.10
  44.3 0.2 all-reduce.4.cloned.1.call-start
  44.6 3.2 %bitcast_convert_fusion = bf16[16,80,768]{2,1,0:T(8,128)(2,1)} fusion(bf16[16,80,3,64]{1,3,2,0:T(8,128)(2,1)} %copy-done.5, bf16[3,64,768]{2,1,0:T(8,128)(2,1)S(1)} %copy-done.8), kind=kOutput, calls=%fused_computation.17 | convolution fusion | flops 378470400 | bytes 2752512 | tf_op jit(solution)/shard_map/zagm,gms->zas/dot_general | solution.py:31
  47.8 0.0 all-reduce.4.cloned.1.call-update
  47.8 0.6 dynamic-slice
  49.1 15.3 %reduce-scatter.9.cloned.1.call-done = f32[96,192]{1,0:T(8,128)} async-done(((f32[768,192]{1,0:T(8,128)}), f32[96,192]{1,0:T(8,128)}) %reduce-scatter.9.cloned.1.call-update) | async-done | bytes 73744
  64.3 1.0 reshape.74
  65.4 0.8 copy.41
  66.1 42.4 %reduce-scatter.7.cloned.1.call-done = f32[96,576]{1,0:T(8,128)} async-done(((f32[768,576]{1,0:T(8,128)}), f32[96,576]{1,0:T(8,128)}) %reduce-scatter.7.cloned.1.call-update) | async-done | bytes 221200
  108.5 1.8 copy.43
  110.3 83.2 %all-reduce.6.cloned.1.call-done = f32[16,80,768]{2,1,0:T(8,128)} async-done(((f32[16,80,768]{2,1,0:T(8,128)}), f32[16,80,768]{2,1,0:T(8,128)}) %all-reduce.6.cloned.1.call-update) | async-done | bytes 3932176 | tf_op jit(solution)/shard_map/psum | solution.py:63
  193.4 3.2 %fusion.11 = (f32[768]{0:T(1024)S(1)}, f32[16,80]{1,0:T(8,128)S(1)}) fusion(f32[16,80,768]{2,1,0:T(8,128)} %all-reduce.6.cloned.1.call-done, bf16[16,80,768]{2,1,0:T(8,128)(2,1)S(1)} %copy-done.1, f32[16,80]{1,0:T(8,128)S(1)} %add_rsqrt_fusion, f32[768]{0:T(1024)S(1)} %copy-done.9), kind=kLoop, calls=%fused_computation.14 | loop fusion | flops 6879232 | bytes 5914624 | tf_op jit(solution)/shard_map/reduce_sum | solution.py:64
  196.7 13.8 %all-reduce = f32[768]{0:T(1024)S(1)} all-reduce(f32[768]{0:T(1024)S(1)} %get-tuple-element.5), channel_id=4, replica_groups=mesh['dp'=8,'mp'=4] {'dp'}, use_global_device_ids=true, to_apply=%region_10.11.clone | all-reduce | flops 768 | bytes 6144
  210.5 0.6 dynamic-slice.1
  211.1 65.9 %all-reduce.4.cloned.1.call-done = bf16[16,80,768]{2,1,0:T(8,128)(2,1)} async-done(((bf16[16,80,768]{2,1,0:T(8,128)(2,1)}), bf16[16,80,768]{2,1,0:T(8,128)(2,1)}) %all-reduce.4.cloned.1.call-update) | async-done | bytes 1966096 | tf_op jit(solution)/shard_map/psum | solution.py:34
  277.0 5.3 %fusion.10 = (bf16[16,80,768]{2,1,0:T(8,128)(2,1)}, bf16[16,80,768]{2,1,0:T(8,128)(2,1)}) fusion(bf16[16,80,768]{2,1,0:T(8,128)(2,1)S(1)} %copy-done.1, f32[16,80,768]{2,1,0:T(8,128)} %all-reduce.6.cloned.1.call-done, f32[16,80]{1,0:T(8,128)S(1)} %broadcast_multiply_fusion, f32[768]{0:T(1024)S(1)} %copy-done.9, f32[16,80]{1,0:T(8,128)S(1)} %add_rsqrt_fusion, ...), kind=kLoop, calls=%fused_computation.13 | loop fusion | flops 12779520 | bytes 13777152 | tf_op jit(solution)/shard_map/convert_element_type | solution.py:67
  (17 shorter events, 0.0 us)
Async XLA Ops:
  8.0 3.0 %copy-start = (bf16[768,3,3,64]{0,3,2,1:T(8,128)(2,1)S(1)}, bf16[768,3,3,64]{0,3,2,1:T(8,128)(2,1)}, u32[]{:S(2)}) copy-start(bf16[768,3,3,64]{0,3,2,1:T(8,128)(2,1)} %param.9) | copy-start | bytes 2654212
  8.0 3.0 %copy-start.1 = (bf16[16,80,768]{2,1,0:T(8,128)(2,1)S(1)}, bf16[16,80,768]{2,1,0:T(8,128)(2,1)}, u32[]{:S(2)}) copy-start(bf16[16,80,768]{2,1,0:T(8,128)(2,1)} %param.6) | copy-start | bytes 5898244
  8.0 3.0 %copy-start.9 = (f32[768]{0:T(1024)S(1)}, f32[768]{0:T(1024)}, u32[]{:S(2)}) copy-start(f32[768]{0:T(1024)} %param.8) | copy-start | bytes 9220
  8.0 56.3 %reduce-scatter.9.cloned.1.call-start = ((), (), s32[]{:S(2)}) async-start(), calls=%async_computation.5 | async-start | bytes 884736
  18.1 3.3 %copy-start.2 = (bf16[16,80,768]{2,1,0:T(8,128)(2,1)S(1)}, bf16[16,80,768]{2,1,0:T(8,128)(2,1)}, u32[]{:S(2)}) copy-start(bf16[16,80,768]{2,1,0:T(8,128)(2,1)} %param.11) | copy-start | bytes 5898244
  20.4 0.9 copy-start.5
  23.8 2.8 copy-start.8
  26.5 82.0 %reduce-scatter.7.cloned.1.call-start = ((), (), s32[]{:S(2)}) async-start(), calls=%async_computation.4 | async-start | bytes 2211840
  26.6 2.6 copy-start.3
  29.2 1.7 copy-start.4
  30.9 2.1 copy-start.11
  32.4 3.6 %copy-start.6 = (bf16[16,80,1,3,64]{1,4,3,0,2:T(8,128)(2,1)}, bf16[16,80,1,3,64]{1,4,3,0,2:T(8,128)(2,1)S(1)}, u32[]{:S(2)}) copy-start(bf16[16,80,1,3,64]{1,4,3,0,2:T(8,128)(2,1)S(1)} %fusion.28) | copy-start | bytes 1474564
  33.0 3.0 %copy-start.7 = (bf16[16,80,1,3,64]{1,4,3,0,2:T(8,128)(2,1)}, bf16[16,80,1,3,64]{1,4,3,0,2:T(8,128)(2,1)S(1)}, u32[]{:S(2)}) copy-start(bf16[16,80,1,3,64]{1,4,3,0,2:T(8,128)(2,1)S(1)} %fusion.29) | copy-start | bytes 1474564
  38.9 154.6 %all-reduce.6.cloned.1.call-start = ((), (), s32[]{:S(2)}) async-start(), calls=%async_computation.3 | async-start | bytes 7864320 | tf_op jit(solution)/shard_map/psum | solution.py:63
  44.3 3.5 %copy-start.10 = (u32[32]{0:T(128)S(1)}, u32[32]{0:T(128)}, u32[]{:S(2)}) copy-start(u32[32]{0:T(128)} %constant.20) | copy-start | bytes 388
  44.3 232.6 %all-reduce.4.cloned.1.call-start = ((), (), s32[]{:S(2)}) async-start(), calls=%async_computation.2 | async-start | bytes 3932160 | tf_op jit(solution)/shard_map/psum | solution.py:34
Sparse Core Ops, SparseCore 0:
  26.6 37.6 reduce-scatter.8
  68.3 40.1 reduce-scatter.6
Sparse Core Ops, SparseCore 1:
  44.4 149.0 all-reduce.5
  196.3 80.6 all-reduce.3
where the time goes:
time: 290 us
  waiting for transfers between devices  207 us (71%)
  matrix products  26.7 us (9%)
  between operations  16.3 us (6%)
  local copies, waits for them, and re-layouts  13.8 us (5%)
  blocking collectives  13.8 us (5%)
  other arithmetic  11.9 us (4%)
    psum x1, waiting for transfers between devices, body(): grad_normed = lax.psum(partial_normed, 'mp')  83.2 us
    psum x1, waiting for transfers between devices, body(): lax.psum(partial_mix.astype(jnp.bfloat16), 'mp').astype(jnp.float32)  65.9 us
    unnamed x6, waiting for transfers between devices  57.7 us
    unnamed x1, blocking collectives  13.8 us
    unnamed x32, local copies, waits for them, and re-layouts  13.8 us
  transfers between devices with their start and end apart: 4, of which 4 were waited for; matrix products, arithmetic and copies ran while one was open for 10% of the time, Pallas kernels for 0%

commit v1 on v0

--- a/solution.py
+++ b/solution.py
@@ -31,7 +31,9 @@
     partial_mix = jnp.einsum(
         "zagm,gms->zas", attended_context, output_weight, preferred_element_type=jnp.float32
     )
-    mixed_total_sum = lax.psum(partial_mix.astype(jnp.bfloat16), "mp").astype(jnp.float32)
+    mixed_total_sum = jnp.sum(
+        lax.all_gather(partial_mix.astype(jnp.bfloat16), "mp"), axis=0
+    ).astype(jnp.float32)
     attended = (wide_states + mixed_total_sum).astype(jnp.bfloat16)
     masked_cotangent = jnp.where(keep_mask[:, :, None], cotangent, jnp.zeros_like(cotangent))
     local_output = jnp.einsum(

time: 290 us -> 353 us (1.22)
  waiting for transfers between devices: 207 us -> 266 us
  other arithmetic: 11.9 us -> 17.5 us
    all_gather x0 -> x1, waiting for transfers between devices: none -> 125 us  [body(): lax.all_gather(partial_mix.astype(jnp.bfloat16), 'mp')]
    psum x1 -> x0, waiting for transfers between devices: 65.9 us -> none  [body(): lax.psum(partial_mix.astype(jnp.bfloat16), 'mp').astype(jnp.float32)]
    reduce_sum x0 -> x1, other arithmetic: none -> 6.21 us  [body(): jnp.sum(lax.all_gather(partial_mix.astype(jnp.bfloat16), 'mp'), axis=0)]
    unnamed x32 -> x34, local copies, waits for them, and re-layouts: 13.8 us -> 13 us
  transfers between devices with their start and end apart: 4 -> 4, of which waited for: 4 -> 4; matrix products, arithmetic and copies ran while one was open for 10% -> 8% of each run, Pallas kernels for 0% -> 0%
where the time goes in v1:
time: 353 us
  waiting for transfers between devices  266 us (75%)
  matrix products  26.8 us (8%)
  other arithmetic  17.5 us (5%)
  between operations  16.3 us (5%)
  blocking collectives  13.4 us (4%)
  local copies, waits for them, and re-layouts  13 us (4%)
    all_gather x1, waiting for transfers between devices, body(): lax.all_gather(partial_mix.astype(jnp.bfloat16), 'mp')  125 us
    psum x1, waiting for transfers between devices, body(): grad_normed = lax.psum(partial_normed, 'mp')  82.5 us
    unnamed x6, waiting for transfers between devices  58.4 us
    unnamed x1, blocking collectives  13.4 us
    unnamed x34, local copies, waits for them, and re-layouts  13 us
  transfers between devices with their start and end apart: 4, of which 4 were waited for; matrix products, arithmetic and copies ran while one was open for 8% of the time, Pallas kernels for 0%

profile of v1, /device:TPU:0, one launch (start us, length us, event | category | flops | bytes accessed | tf_op | source)
XLA Modules:
  0.0 353.0 jit_solution(12529718057468380364)
XLA Ops:
  8.0 0.0 copy-start
  8.0 0.0 copy-start.1
  8.0 0.0 reduce-scatter.9.cloned.1.call-start
  8.1 2.2 fusion.12
  10.3 0.1 iota_compare_fusion
  10.4 0.1 copy-done.1
  10.4 3.4 convolution_convert_fusion
  13.9 3.6 %fusion.51 = (f32[16,3,80]{2,1,0:T(4,128)S(1)}, f32[16,3,80,80]{2,3,1,0:T(8,128)}) fusion(pred[16,80]{1,0:T(8,128)(4,1)S(1)} %iota_compare_fusion, bf16[16,80,3,3,64]{1,4,3,2,0:T(8,128)(2,1)} %convolution_convert_fusion), kind=kOutput, calls=%fused_computation.69 | convolution fusion | flops 40243280 | bytes 2818304 | tf_op jit(solution)/shard_map/sub | solution.py:25
  17.5 2.3 fusion.27
  19.8 0.9 copy-done.5
  20.7 0.9 fusion.31
  21.6 1.5 copy.40
  23.1 2.7 reshape.74
  25.8 0.0 reduce-scatter.9.cloned.1.call-update
  25.9 0.0 reduce-scatter.7.cloned.1.call-start
  25.9 0.0 copy-start.3
  26.0 2.6 fusion.24
  28.6 0.2 copy-done.4
  28.8 0.6 multiply_reduce_fusion
  29.4 0.6 fusion.30
  30.1 0.0 copy-start.12
  30.1 0.5 multiply_convert_fusion
  30.5 0.4 fusion.28
  31.0 0.6 fusion.29
  31.6 0.0 copy-done.12
  31.6 3.0 fusion.14
  34.6 2.8 copy.42
  37.4 0.0 reduce-scatter.7.cloned.1.call-update
  37.4 0.0 all-reduce.3.cloned.1.call-start
  37.5 5.5 %convolution_bitcast_fusion = f32[16,80,768]{2,1,0:T(8,128)} fusion(bf16[16,80,1,3,64]{1,4,3,0,2:T(8,128)(2,1)} %copy-done.12, bf16[16,80,1,3,64]{1,4,3,0,2:T(8,128)(2,1)} %copy-done.7, bf16[16,80,1,3,64]{1,4,3,0,2:T(8,128)(2,1)} %copy-done.6, bf16[768,3,3,64]{0,3,2,1:T(8,128)(2,1)S(1)} %copy-done), kind=kOutput, calls=%fused_computation.19 | convolution fusion | flops 1133936640 | bytes 6291456 | tf_op jit(solution)/shard_map/bschk,dchk->bsd/dot_general | solution.py:61
  43.0 0.0 all-reduce.3.cloned.1.call-update
  43.0 0.0 copy-start.11
  43.0 0.2 all-gather.3.cloned.1.call-start
  43.2 3.2 bitcast_convert_fusion
  46.4 0.0 all-gather.3.cloned.1.call-update
  46.5 0.6 dynamic-slice
  47.7 16.0 %reduce-scatter.9.cloned.1.call-done = f32[96,192]{1,0:T(8,128)} async-done(((f32[768,192]{1,0:T(8,128)}), f32[96,192]{1,0:T(8,128)}) %reduce-scatter.9.cloned.1.call-update) | async-done | bytes 73744
  63.7 1.0 reshape.75
  64.7 0.8 copy.41
  65.4 42.4 %reduce-scatter.7.cloned.1.call-done = f32[96,576]{1,0:T(8,128)} async-done(((f32[768,576]{1,0:T(8,128)}), f32[96,576]{1,0:T(8,128)}) %reduce-scatter.7.cloned.1.call-update) | async-done | bytes 221200
  107.8 1.8 copy.43
  109.7 82.5 %all-reduce.3.cloned.1.call-done = f32[16,80,768]{2,1,0:T(8,128)} async-done(((f32[16,80,768]{2,1,0:T(8,128)}), f32[16,80,768]{2,1,0:T(8,128)}) %all-reduce.3.cloned.1.call-update) | async-done | bytes 3932176 | tf_op jit(solution)/shard_map/psum | solution.py:65
  192.1 3.2 fusion.11
  195.4 13.4 %all-reduce = f32[768]{0:T(1024)S(1)} all-reduce(f32[768]{0:T(1024)S(1)} %get-tuple-element.5), channel_id=5, replica_groups=mesh['dp'=8,'mp'=4] {'dp'}, use_global_device_ids=true, to_apply=%region_10.11.clone | all-reduce | flops 768 | bytes 6144
  208.8 0.6 dynamic-slice.1
  209.4 124.7 %all-gather.3.cloned.1.call-done = bf16[64,80,768]{2,1,0:T(8,128)(2,1)} async-done(((bf16[16,80,768]{2,1,0:T(8,128)(2,1)}), bf16[64,80,768]{2,1,0:T(8,128)(2,1)}) %all-gather.3.cloned.1.call-update) | async-done | bytes 7864336 | tf_op jit(solution)/shard_map/all_gather | solution.py:35
  334.1 6.2 %reduce_sum.59 = bf16[16,80,768]{2,1,0:T(8,128)(2,1)} reduce(bf16[4,16,80,768]{3,2,1,0:T(8,128)(2,1)} %bitcast.105, bf16[]{:T(256)} %constant.16.clone.1), dimensions={0}, to_apply=%region_3.4 | reduce | flops 2949120 | bytes 9830402 | tf_op jit(solution)/shard_map/reduce_sum | solution.py:34
  340.3 5.3 %fusion.10 = (bf16[16,80,768]{2,1,0:T(8,128)(2,1)}, bf16[16,80,768]{2,1,0:T(8,128)(2,1)}) fusion(bf16[16,80,768]{2,1,0:T(8,128)(2,1)S(1)} %copy-done.1, f32[16,80,768]{2,1,0:T(8,128)} %all-reduce.3.cloned.1.call-done, f32[16,80]{1,0:T(8,128)S(1)} %broadcast_multiply_fusion, f32[768]{0:T(1024)S(1)} %copy-done.9, f32[16,80]{1,0:T(8,128)S(1)} %add_rsqrt_fusion, ...), kind=kLoop, calls=%fused_computation.13 | loop fusion | flops 12779520 | bytes 13777152 | tf_op jit(solution)/shard_map/convert_element_type | solution.py:69
  (20 shorter events, 0.0 us)
Async XLA Ops:
  8.0 2.4 copy-start
  8.0 2.4 copy-start.1
  8.0 2.3 copy-start.10
  8.0 2.4 copy-start.9
  8.0 55.6 %reduce-scatter.9.cloned.1.call-start = ((), (), s32[]{:S(2)}) async-start(), calls=%async_computation.5 | async-start | bytes 884736
  17.4 3.3 copy-start.2
  19.8 0.9 copy-start.5
  23.1 2.8 copy-start.8
  25.9 82.0 %reduce-scatter.7.cloned.1.call-start = ((), (), s32[]{:S(2)}) async-start(), calls=%async_computation.4 | async-start | bytes 2211840
  25.9 2.6 copy-start.3
  25.9 2.8 copy-start.4
  30.1 1.5 copy-start.12
  30.9 3.6 %copy-start.6 = (bf16[16,80,1,3,64]{1,4,3,0,2:T(8,128)(2,1)}, bf16[16,80,1,3,64]{1,4,3,0,2:T(8,128)(2,1)S(1)}, u32[]{:S(2)}) copy-start(bf16[16,80,1,3,64]{1,4,3,0,2:T(8,128)(2,1)S(1)} %fusion.28) | copy-start | bytes 1474564
  31.6 3.0 copy-start.7
  37.4 154.7 %all-reduce.3.cloned.1.call-start = ((), (), s32[]{:S(2)}) async-start(), calls=%async_computation.2 | async-start | bytes 7864320 | tf_op jit(solution)/shard_map/psum | solution.py:65
  43.0 3.5 copy-start.11
  43.0 291.1 %all-gather.3.cloned.1.call-start = ((), (), s32[]{:S(2)}) async-start(), calls=%async_computation.3 | async-start | bytes 9830400 | tf_op jit(solution)/shard_map/all_gather | solution.py:35
Sparse Core Ops, SparseCore 0:
  26.0 37.6 reduce-scatter.8
  67.7 40.1 reduce-scatter.6
Sparse Core Ops, SparseCore 1:
  43.1 149.0 all-reduce.2
  194.2 139.9 all-gather.2
